TPU v7x, 32 devices: a whole 2x2x4 slice. The times are simulated.
32 devices in a mesh: member: 4 (over y, x), tile: 8 (over z, core).
Axes of the slice: x: 2, y: 2, z: 4, core: 2. Of those that a mesh axis runs over, the one named last changes fastest.
Arguments:
- northward_speed_field: float32 [16, 16, 64, 256], P('member', None, 'tile'), may hold values from -6 to 6
- level_depth_extent: float32 [16, 16, 64, 256], P('member', None, 'tile'), may hold values from 0.2 to 5
- potential_warmth_anomaly: float32 [16, 16, 64, 256], P('member', None, 'tile'), may hold values from -6 to 6
- ocean_region_label: int32 [64, 256], P('tile'), may hold values from 0 to 9
- zone_for_parallel: int32 [256], replicated, may hold values from 0 to 15, never falling along the last dimension, each value on 1 to 32 neighbouring positions
Outputs:
- mean_psi: float32 [10, 16, 256], P(None, None, ('member', 'tile'))
- mean_heat: float32 [10, 256], P(None, ('member', 'tile'))
- covariance: float32 [16, 16, 16], replicated
Inputs may be any that keep to these rules, and one draw needn't show every extreme that they name: `zone_for_parallel`: never falls along latitude; every band holds 1 to 32 latitudes.
All inputs are finite; a program needn't handle non-finite values.
Results may differ from a plain program's by a relative error of at most 0.00011.
Values sent between devices are 32-bit elements; how exact they have to be, the bound alone decides.
No kernel may reach another device: no remote copies, remote signals or barrier semaphores. Data moves between devices by JAX's collectives and lax.ppermute only.
A program may use at most 128 MiB of HBM per device.

v0:
```python
import math
import jax
import jax.numpy as jnp
from jax import lax
from jax.sharding import PartitionSpec as P

BASINS = 10
NBANDS = 16


def metric_factor(lats):
    index = jnp.arange(lats, dtype=jnp.float32)
    return jnp.cos((-80.0 + 160.0 * (index + 0.5) / lats) * (math.pi / 180.0))


def local(
    northward_speed_field,
    level_depth_extent,
    potential_warmth_anomaly,
    ocean_region_label,
    zone_for_parallel,
):
    greatest_bound_value = lax.Precision.HIGHEST
    members_here, layers, columns, lats = northward_speed_field.shape
    tiles = lax.axis_size("tile")
    groups = lax.axis_size("member")
    owned = lats // (groups * tiles)
    northward_volume_carriage = northward_speed_field * level_depth_extent * metric_factor(lats)
    region_indicator_matrix = (
        ocean_region_label[None, :, :] == jnp.arange(BASINS, dtype=jnp.int32)[:, None, None]
    ).astype(jnp.float32)
    transport = jnp.einsum(
        "mkxl,bxl->mbkl",
        northward_volume_carriage,
        region_indicator_matrix,
        precision=greatest_bound_value,
    ) / math.sqrt(columns * tiles)
    thermal_energy_integral = jnp.einsum(
        "tzux,pux->tpx",
        northward_volume_carriage * potential_warmth_anomaly,
        region_indicator_matrix,
        precision=greatest_bound_value,
    ) / math.sqrt(columns * tiles * layers)
    partial_value = jnp.concatenate(
        [transport.reshape(members_here, BASINS * layers, lats), thermal_energy_integral], axis=1
    )
    regrouped = lax.all_to_all(partial_value, "member", split_axis=2, concat_axis=0, tiled=True)
    summed = lax.psum_scatter(regrouped, "tile", scatter_dimension=2, tiled=True)
    members = summed.shape[0]
    streams = jnp.cumsum(
        summed[:, : BASINS * layers].reshape(members, BASINS, layers, owned), axis=2
    )
    heat_all = summed[:, BASINS * layers :]
    mean_psi = jnp.mean(streams, axis=0)
    mean_heat = jnp.mean(heat_all, axis=0)
    anomaly = (streams - mean_psi).reshape(members, BASINS * layers, owned)
    start = (lax.axis_index("member") * tiles + lax.axis_index("tile")) * owned
    bands_here = lax.dynamic_slice_in_dim(zone_for_parallel, start, owned)
    band_hot = (bands_here[:, None] == jnp.arange(NBANDS, dtype=jnp.int32)[None, :]).astype(
        jnp.float32
    )
    products = jnp.einsum("mfl,nfl->lmn", anomaly, anomaly, precision=greatest_bound_value)
    norm = float((members - 1) * BASINS * layers * (lats // NBANDS))
    local_cov = jnp.einsum("lmn,lc->cmn", products, band_hot, precision=greatest_bound_value) / norm
    covariance = lax.psum(local_cov, ("member", "tile"))
    return (mean_psi, mean_heat, covariance)


def solution(mesh):
    in_specs = (
        P("member", None, "tile", None),
        P("member", None, "tile", None),
        P("member", None, "tile", None),
        P("tile", None),
        P(),
    )
    out_specs = (P(None, None, ("member", "tile")), P(None, ("member", "tile")), P())
    return jax.shard_map(local, mesh=mesh, in_specs=in_specs, out_specs=out_specs, check_vma=False)
```

profile of v0, /device:TPU:10, one launch (start us, length us, event | category | flops | bytes accessed | tf_op | source)
XLA Modules:
  0.0 139.2 jit_solution(16982006335386744213)
XLA Ops:
  7.2 0.0 reduce-scatter.2.cloned.1.call-start
  7.3 1.5 %multiply_reduce_fusion = (f32[4,8,256]{2,1,0:T(8,128)S(1)}, f32[4,16,8,256]{3,2,1,0:T(8,128)S(1)}) fusion(f32[4,16,8,256]{3,2,1,0:T(8,128)} %param.7, f32[256]{0:T(256)S(1)} %multiply_cosine_fusion, f32[4,16,8,256]{3,2,1,0:T(8,128)} %param.5, f32[4,16,8,256]{3,2,1,0:T(8,128)} %param.6), kind=kLoop, calls=%fused_computation.7 | loop fusion | flops 516096 | bytes 2130944 | tf_op jit(solution)/shard_map/tzux,pux->tpx/reduce_sum | solution.py:38
  8.7 4.4 %copy.34 = f32[4,16,8,256]{1,2,0,3:T(8,128)} copy(f32[4,16,8,256]{3,2,1,0:T(8,128)S(1)} %get-tuple-element.16) | data formatting | bytes 1048576 | tf_op jit(solution)/shard_map/mul | solution.py:28
  13.1 0.1 copy.33
  13.2 9.7 %multiply_bitcast_fusion = f32[4,10,16,256]{2,1,0,3:T(8,128)} fusion(f32[4,16,8,256]{1,2,0,3:T(8,128)} %copy.34, s32[8,256]{0,1:T(8,128)S(1)} %copy.33), kind=kOutput, calls=%fused_computation | convolution fusion | flops 15912960 | bytes 1187840 | tf_op jit(solution)/shard_map/mkxl,bxl->mbkl/dot_general | solution.py:32
  22.9 5.3 %copy.35 = f32[4,10,16,256]{3,2,1,0:T(8,128)S(1)} copy(f32[4,10,16,256]{2,1,0,3:T(8,128)} %multiply_bitcast_fusion) | data formatting | bytes 1310720 | tf_op jit(solution)/shard_map/div | solution.py:32
  28.2 0.2 copy.36
  28.4 1.1 fusion
  29.5 0.2 copy.37
  29.7 0.1 pad_maximum_fusion
  29.8 0.4 copy.38
  30.2 17.1 %all_to_all.18 = f32[4,170,256]{1,0,2:T(4,128)S(1)} all-to-all(f32[4,170,256]{1,0,2:T(4,128)S(1)} %copy.38), channel_id=1, replica_groups=mesh['member'=4,'tile'=8] {'member'}, dimensions={2} | all-to-all | bytes 1392640 | tf_op jit(solution)/shard_map/all_to_all | solution.py:47
  47.3 0.2 copy.39
  47.5 1.1 copy.40
  48.6 0.0 reduce-scatter.2.cloned.1.call-update
  48.6 0.1 dynamic_slice.3
  48.7 29.1 %reduce-scatter.2.cloned.1.call-done = f32[16,170,8]{1,2,0:T(8,128)} async-done(((f32[16,170,64]{1,2,0:T(8,128)}), f32[16,170,8]{1,2,0:T(8,128)}) %reduce-scatter.2.cloned.1.call-update) | async-done | bytes 87056 | tf_op jit(solution)/shard_map/reduce_scatter | solution.py:48
  77.8 1.2 reshape.33
  79.0 2.3 %copy.41 = f32[16,10,16,8]{3,1,2,0:T(8,128)} copy(f32[16,10,16,8]{2,1,3,0:T(8,128)S(1)} %reshape.33) | data formatting | bytes 163840 | tf_op jit(solution)/shard_map/reshape | solution.py:51
  81.3 1.8 %fusion.11 = f32[16,10,16,8]{3,1,2,0:T(8,128)S(1)} fusion(f32[16,10,16,8]{3,1,2,0:T(8,128)} %copy.41), kind=kOutput, calls=%fused_computation.22 | output fusion | flops 307200 | bytes 163840 | tf_op jit(solution)/shard_map/jit(cumsum)/reduce_window_sum | solution.py:50
  83.1 1.1 copy.42
  84.2 0.2 reduce_sum.28
  84.4 0.1 copy.43
  84.5 0.7 copy.47
  85.2 0.1 div.54
  85.3 0.3 reduce_window_sum.14
  85.6 0.3 fusion.5
  85.9 0.3 convolution_multiply_fusion.1
  86.3 44.7 %psum.7 = f32[16,16,16]{2,0,1:T(8,128)S(1)} all-reduce(f32[16,16,16]{2,0,1:T(8,128)S(1)} %convolution_multiply_fusion.1), channel_id=1, replica_groups=mesh['member'=4,'tile'=8] {'member','tile'}, use_global_device_ids=true, to_apply=%region_5.6 | all-reduce | flops 4096 | bytes 32768 | tf_op jit(solution)/shard_map/psum | solution.py:65
  131.0 0.7 copy.48
  131.7 0.1 slice_reduce_fusion
  131.8 0.6 broadcast_multiply_fusion.1
  (9 shorter events, 0.1 us)
Async XLA Ops:
  7.2 5.9 %copy-start.1 = (s32[8,256]{1,0:T(8,128)S(1)}, s32[8,256]{1,0:T(8,128)}, u32[]{:S(2)}) copy-start(s32[8,256]{1,0:T(8,128)} %param.8) | copy-start | bytes 24580
  7.2 70.6 %reduce-scatter.2.cloned.1.call-start = ((), (), s32[]{:S(2)}) async-start(), calls=%async_computation.2 | async-start | bytes 1179648 | tf_op jit(solution)/shard_map/reduce_scatter | solution.py:48
  29.8 18.8 %copy-start.2 = (s32[256]{0:T(256)S(1)}, s32[256]{0:T(256)}, u32[]{:S(2)}) copy-start(s32[256]{0:T(256)} %param.9) | copy-start | bytes 3076
  83.1 48.6 %copy-start = (f32[16,170,8]{1,2,0:T(8,128)S(1)}, f32[16,170,8]{1,2,0:T(8,128)}, u32[]{:S(2)}) copy-start(f32[16,170,8]{1,2,0:T(8,128)} %reduce-scatter.2.cloned.1.call-done) | copy-start | bytes 261124
Sparse Core Ops, SparseCore 0:
  48.7 29.0 reduce-scatter.1
where the time goes:
time: 140 us; the launch traced here: 139 us
  blocking collectives  61.8 us (44%)
  waiting for transfers between devices  29.1 us (21%)
  local copies, waits for them, and re-layouts  18.4 us (13%)
  between operations  14.2 us (10%)
  matrix products  11.3 us (8%)
  other arithmetic  4.26 us (3%)
    psum x1, blocking collectives, local(): covariance = lax.psum(local_cov, ('member', 'tile'))  44.7 us
    reduce_scatter x1, waiting for transfers between devices, local(): lax.psum_scatter(regrouped, 'tile', scatter_dimension=2, tiled=True)  29.1 us
    all_to_all x1, blocking collectives, local(): lax.all_to_all(partial_value, 'member', split_axis=2, concat_axis=0, tile...  17.1 us
    dot_general x1, matrix products, local(): jnp.einsum('mkxl,bxl->mbkl', northward_volume_carriage, region_indicator_...  9.66 us
    div x1, local copies, waits for them, and re-layouts, local(): jnp.einsum('mkxl,bxl->mbkl', northward_volume_carriage, region_indicator_...  5.26 us
    mul x1, local copies, waits for them, and re-layouts, local(): northward_speed_field * level_depth_extent * metric_factor(lats)  4.36 us
    reshape x2, local copies, waits for them, and re-layouts, local(): summed[:, :BASINS * layers].reshape(members, BASINS, layers, owned)  3.48 us
  transfers between devices with their start and end apart: 1, of which 1 were waited for; matrix products, arithmetic and copies ran while one was open for 0% of the time, Pallas kernels for 0%

commit v1 on v0

--- a/solution.py
+++ b/solution.py
@@ -62,7 +62,12 @@
     products = jnp.einsum("mfl,nfl->lmn", anomaly, anomaly, precision=greatest_bound_value)
     norm = float((members - 1) * BASINS * layers * (lats // NBANDS))
     local_cov = jnp.einsum("lmn,lc->cmn", products, band_hot, precision=greatest_bound_value) / norm
-    covariance = lax.psum(local_cov, ("member", "tile"))
+
+    def _see_sheet(xin, lane_axis):
+        step_out = jnp.sum(lax.all_gather(xin, lane_axis), 0)
+        return step_out
+
+    covariance = _see_sheet(local_cov, ("member", "tile"))
     return (mean_psi, mean_heat, covariance)
 
 

time: 140 us -> 168 us (1.20)
  the two profiles are of different devices: /device:TPU:10 before, /device:TPU:0 now
where the time goes in v1:
time: 168 us
  blocking collectives  84.7 us (50%)
  waiting for transfers between devices  32.4 us (19%)
  local copies, waits for them, and re-layouts  18.4 us (11%)
  between operations  14.2 us (8%)
  matrix products  11.3 us (7%)
  other arithmetic  6.74 us (4%)
    all_gather x1, blocking collectives, _see_sheet(): step_out = jnp.sum(lax.all_gather(xin, lane_axis), 0)  65.5 us
    reduce_scatter x1, waiting for transfers between devices, local(): lax.psum_scatter(regrouped, 'tile', scatter_dimension=2, tiled=True)  32.4 us
    all_to_all x1, blocking collectives, local(): lax.all_to_all(partial_value, 'member', split_axis=2, concat_axis=0, tile...  19.1 us
    dot_general x1, matrix products, local(): jnp.einsum('mkxl,bxl->mbkl', northward_volume_carriage, region_indicator_...  9.66 us
    div x1, local copies, waits for them, and re-layouts, local(): jnp.einsum('mkxl,bxl->mbkl', northward_volume_carriage, region_indicator_...  5.26 us
    mul x1, local copies, waits for them, and re-layouts, local(): northward_speed_field * level_depth_extent * metric_factor(lats)  4.36 us
    reshape x2, local copies, waits for them, and re-layouts, local(): summed[:, :BASINS * layers].reshape(members, BASINS, layers, owned)  3.48 us
  transfers between devices with their start and end apart: 1, of which 1 were waited for; matrix products, arithmetic and copies ran while one was open for 0% of the time, Pallas kernels for 0%

profile of v1, /device:TPU:0, one launch (start us, length us, event | category | flops | bytes accessed | tf_op | source)
XLA Modules:
  0.0 167.8 jit_solution(10977340683092625910)
XLA Ops:
  7.2 0.0 reduce-scatter.2.cloned.1.call-start
  7.3 1.5 multiply_reduce_fusion
  8.7 4.4 %copy.31 = f32[4,16,8,256]{1,2,0,3:T(8,128)} copy(f32[4,16,8,256]{3,2,1,0:T(8,128)S(1)} %get-tuple-element.7) | data formatting | bytes 1048576 | tf_op jit(solution)/shard_map/mul | solution.py:28
  13.1 0.1 copy.30
  13.2 9.7 %multiply_bitcast_fusion = f32[4,10,16,256]{2,1,0,3:T(8,128)} fusion(f32[4,16,8,256]{1,2,0,3:T(8,128)} %copy.31, s32[8,256]{0,1:T(8,128)S(1)} %copy.30), kind=kOutput, calls=%fused_computation | convolution fusion | flops 15912960 | bytes 1187840 | tf_op jit(solution)/shard_map/mkxl,bxl->mbkl/dot_general | solution.py:32
  22.9 5.3 %copy.32 = f32[4,10,16,256]{3,2,1,0:T(8,128)S(1)} copy(f32[4,10,16,256]{2,1,0,3:T(8,128)} %multiply_bitcast_fusion) | data formatting | bytes 1310720 | tf_op jit(solution)/shard_map/div | solution.py:32
  28.2 0.2 copy.33
  28.4 1.1 fusion
  29.5 0.2 copy.34
  29.7 0.1 pad_maximum_fusion
  29.8 0.4 copy.35
  30.2 19.1 %all_to_all.18 = f32[4,170,256]{1,0,2:T(4,128)S(1)} all-to-all(f32[4,170,256]{1,0,2:T(4,128)S(1)} %copy.35), channel_id=1, replica_groups=mesh['member'=4,'tile'=8] {'member'}, dimensions={2} | all-to-all | bytes 1392640 | tf_op jit(solution)/shard_map/all_to_all | solution.py:47
  49.3 0.2 copy.36
  49.5 1.1 copy.37
  50.6 0.1 dynamic_slice.3
  50.7 32.4 %reduce-scatter.2.cloned.1.call-done = f32[16,170,8]{1,2,0:T(8,128)} async-done(((f32[16,170,64]{1,2,0:T(8,128)}), f32[16,170,8]{1,2,0:T(8,128)}) %reduce-scatter.2.cloned.1.call-update) | async-done | bytes 87056 | tf_op jit(solution)/shard_map/reduce_scatter | solution.py:48
  83.1 1.2 reshape.33
  84.3 2.3 %copy.38 = f32[16,10,16,8]{3,1,2,0:T(8,128)} copy(f32[16,10,16,8]{2,1,3,0:T(8,128)S(1)} %reshape.33) | data formatting | bytes 163840 | tf_op jit(solution)/shard_map/reshape | solution.py:51
  86.6 1.8 %fusion.11 = f32[16,10,16,8]{3,1,2,0:T(8,128)S(1)} fusion(f32[16,10,16,8]{3,1,2,0:T(8,128)} %copy.38), kind=kOutput, calls=%fused_computation.22 | output fusion | flops 307200 | bytes 163840 | tf_op jit(solution)/shard_map/jit(cumsum)/reduce_window_sum | solution.py:50
  88.4 1.1 copy.39
  89.5 0.2 reduce_sum.37
  89.7 0.1 copy.40
  89.8 0.7 copy.44
  90.5 0.1 div.54
  90.6 0.3 reduce_window_sum.14
  90.9 0.3 fusion.5
  91.2 0.3 convolution_multiply_fusion.1
  91.5 65.5 %all-gather = f32[512,16,16]{2,0,1:T(8,128)} all-gather(f32[16,16,16]{2,0,1:T(8,128)S(1)} %convolution_multiply_fusion.1), channel_id=2, replica_groups=mesh['member'=4,'tile'=8] {'member','tile'}, dimensions={0}, use_global_device_ids=true | all-gather | bytes 540672 | tf_op jit(solution)/shard_map/all_gather | solution.py:67
  157.1 2.5 %reduce_sum.39 = f32[16,16,16]{2,0,1:T(8,128)S(1)} reduce(f32[32,16,16,16]{3,1,0,2:T(8,128)} %bitcast.28, f32[]{:T(128)} %constant.13.clone.1), dimensions={0}, to_apply=%region_5.6 | reduce | flops 126976 | bytes 540676 | tf_op jit(solution)/shard_map/reduce_sum | solution.py:67
  159.6 0.7 copy.45
  160.3 0.1 slice_reduce_fusion
  160.3 0.6 broadcast_multiply_fusion.1
  (10 shorter events, 0.1 us)
Async XLA Ops:
  7.2 5.9 %copy-start.1 = (s32[8,256]{1,0:T(8,128)S(1)}, s32[8,256]{1,0:T(8,128)}, u32[]{:S(2)}) copy-start(s32[8,256]{1,0:T(8,128)} %param.8) | copy-start | bytes 24580
  7.2 75.9 %reduce-scatter.2.cloned.1.call-start = ((), (), s32[]{:S(2)}) async-start(), calls=%async_computation.2 | async-start | bytes 1179648 | tf_op jit(solution)/shard_map/reduce_scatter | solution.py:48
  29.8 20.9 %copy-start.2 = (s32[256]{0:T(256)S(1)}, s32[256]{0:T(256)}, u32[]{:S(2)}) copy-start(s32[256]{0:T(256)} %param.9) | copy-start | bytes 3076
  91.5 68.7 %copy-start = (f32[16,170,8]{1,2,0:T(8,128)S(1)}, f32[16,170,8]{1,2,0:T(8,128)}, u32[]{:S(2)}) copy-start(f32[16,170,8]{1,2,0:T(8,128)} %reduce-scatter.2.cloned.1.call-done) | copy-start | bytes 261124
Sparse Core Ops, SparseCore 0:
  50.7 32.3 reduce-scatter.1
